TPU v7x, 32 devices: a whole 2x2x4 slice. The times are simulated.
32 devices in a mesh: row: 8 (over z, y), col: 4 (over x, core).
Axes of the slice: x: 2, y: 2, z: 4, core: 2. Of those that a mesh axis runs over, the one named last changes fastest.
Arguments:
- densities: bfloat16 [4608, 3072], P(('row', 'col')), may hold values from -0.796875 to 0.796875
- counts: int32 [512], P(('row', 'col')), may hold values from 3 to 9
- coulomb: float32 [3072], replicated, may hold values from 0.05 to 1
- energies: float32 [4608], P(('row', 'col')), may hold values from 8 to 64
- vectors: bfloat16 [4608, 64], P(('row', 'col')), may hold values from -0.09375 to 0.09375
Outputs:
- kernel: float32 [4608, 4608], P('row', 'col')
- product: float32 [4608, 64], P(('row', 'col'))
All inputs are finite; a program needn't handle non-finite values.
Results may differ from a plain program's by a relative error of at most 0.0095.
Values may be sent and summed in bfloat16 or wider, within the bound.
A program may use at most 128 MiB of HBM per device.

v0:
```python
import jax
import jax.numpy as jnp
from jax import lax
from jax.sharding import PartitionSpec as P

SLOT = 9


def body(densities, counts, coulomb, energies, vectors):
    kpoints = counts.shape[0]
    slot_index = lax.broadcasted_iota(jnp.int32, (kpoints, SLOT), 1)
    usable = (slot_index < counts[:, None]).reshape(kpoints * SLOT)
    masked = jnp.where(usable[:, None], densities, jnp.zeros_like(densities))
    weighted = (masked.astype(jnp.float32) * coulomb[None, :]).astype(jnp.bfloat16)
    row_block = lax.all_gather(weighted, "col", axis=0, tiled=True)
    kernel = lax.dot_general(
        row_block,
        lax.all_gather(masked, "row", axis=0, tiled=True),
        (((1,), (1,)), ((), ())),
        preferred_element_type=jnp.float32,
    )
    local_terms = lax.dot_general(
        masked, vectors, (((0,), (0,)), ((), ())), preferred_element_type=jnp.float32
    )
    projected = lax.psum(local_terms, ("row", "col"))
    coupled = jnp.dot(
        weighted.astype(jnp.float32),
        projected,
        precision=lax.Precision.HIGHEST,
        preferred_element_type=jnp.float32,
    )
    diagonal = jnp.where(usable, energies, jnp.zeros_like(energies))
    product = coupled + diagonal[:, None] * vectors.astype(jnp.float32)
    return (kernel, product)


def solution(mesh):
    return jax.shard_map(
        body,
        mesh=mesh,
        in_specs=(
            P(("row", "col"), None),
            P(("row", "col")),
            P(),
            P(("row", "col")),
            P(("row", "col"), None),
        ),
        out_specs=(P("row", "col"), P(("row", "col"), None)),
        check_vma=False,
    )
```

profile of v0, /device:TPU:0, one launch (start us, length us, event | category | flops | bytes accessed | tf_op | source)
XLA Modules:
  0.0 254.9 jit_solution(2723518301834246498)
XLA Ops:
  8.0 0.0 copy-start.2
  8.0 0.0 all-reduce.2.cloned.1.call-start
  8.1 0.7 iota_compare_fusion
  8.8 0.1 lt.18
  8.9 2.5 multiply_convert_fusion
  11.4 0.0 copy-start
  11.4 0.0 copy-done.2
  11.4 0.0 copy-start.3
  11.4 0.0 copy-start.1
  11.4 1.8 fusion.1
  13.2 0.0 all-reduce.2.cloned.1.call-update
  13.2 0.0 all-gather.3.cloned.1.call-start
  13.3 0.5 all-gather.3.cloned.1.call-update
  13.8 0.0 all-gather.5.cloned.1.call-start
  13.9 0.0 copy-done
  13.9 0.5 all-gather.5.cloned.1.call-update
  14.4 0.0 copy-done.3
  14.4 219.2 %all-reduce.2.cloned.1.call-done = f32[3072,64]{1,0:T(8,128)} async-done(((f32[3072,64]{1,0:T(8,128)}), f32[3072,64]{1,0:T(8,128)}) %all-reduce.2.cloned.1.call-update) | async-done | bytes 786448 | tf_op jit(solution)/shard_map/psum | solution.py:25
  233.7 0.0 copy-done.1
  233.7 3.5 %convolution_add_fusion = f32[144,64]{0,1:T(8,128)} fusion(bf16[144,3072]{1,0:T(8,128)(2,1)S(1)} %copy-done.1, f32[3072,64]{1,0:T(8,128)} %all-reduce.2.cloned.1.call-done, bf16[144,64]{0,1:T(8,128)(2,1)S(1)} %copy-done.2, f32[144]{0:T(256)S(1)} %broadcast_select_fusion.1), kind=kOutput, calls=%fused_computation.1 | convolution fusion | flops 339766272 | bytes 1727040 | tf_op jit(solution)/shard_map/dot_general | solution.py:26
  237.1 0.0 all-gather.3.cloned.1.call-done
  237.1 0.0 all-gather.5.cloned.1.call-done
  237.1 10.4 %fusion = f32[576,1152]{1,0:T(8,128)} fusion(bf16[576,3072]{1,0:T(8,128)(2,1)} %all-gather.3.cloned.1.call-done, bf16[1152,3072]{1,0:T(8,128)(2,1)} %all-gather.5.cloned.1.call-done), kind=kOutput, calls=%fused_computation.5 | convolution fusion | flops 4076863488 | bytes 13271040 | tf_op jit(solution)/shard_map/dot_general | solution.py:16
  (1 shorter events, 0.0 us)
Async XLA Ops:
  8.0 3.4 %copy-start.2 = (bf16[144,64]{0,1:T(8,128)(2,1)S(1)}, bf16[144,64]{0,1:T(8,128)(2,1)}, u32[]{:S(2)}) copy-start(bf16[144,64]{0,1:T(8,128)(2,1)} %param.9) | copy-start | bytes 55300
  8.0 225.6 %all-reduce.2.cloned.1.call-start = ((), (), s32[]{:S(2)}) async-start(), calls=%async_computation.2 | async-start | bytes 3145728 | tf_op jit(solution)/shard_map/psum | solution.py:25
  11.4 2.5 copy-start
  11.4 3.0 %copy-start.3 = (f32[144]{0:T(256)S(1)}, f32[144]{0:T(256)}, u32[]{:S(2)}) copy-start(f32[144]{0:T(256)} %param.8) | copy-start | bytes 1732
  11.4 222.2 %copy-start.1 = (bf16[144,3072]{1,0:T(8,128)(2,1)S(1)}, bf16[144,3072]{1,0:T(8,128)(2,1)}, u32[]{:S(2)}) copy-start(bf16[144,3072]{1,0:T(8,128)(2,1)} %get-tuple-element.2) | copy-start | bytes 2654212
  13.2 223.9 %all-gather.3.cloned.1.call-start = ((), (), s32[]{:S(2)}) async-start(), calls=%async_computation | async-start | bytes 4423680 | tf_op jit(solution)/shard_map/all_gather | solution.py:15
  13.8 223.3 %all-gather.5.cloned.1.call-start = ((), (), s32[]{:S(2)}) async-start(), calls=%async_computation.1 | async-start | bytes 7962624 | tf_op jit(solution)/shard_map/all_gather | solution.py:18
Sparse Core Ops, SparseCore 0:
  14.7 218.9 all-reduce.1
Sparse Core Ops, SparseCore 1:
  15.3 34.0 all-gather.2
  51.4 109.7 all-gather.4
where the time goes:
time: 255 us
  waiting for transfers between devices  220 us (86%)
  matrix products  15.6 us (6%)
  between operations  15.5 us (6%)
  other arithmetic  3.27 us (1%)
    psum x1, waiting for transfers between devices, body(): projected = lax.psum(local_terms, ('row', 'col'))  219 us
    dot_general x1, matrix products, body(): lax.dot_general(row_block, lax.all_gather(masked, 'row', axis=0, tiled=Tr...  10.4 us
  transfers between devices with their start and end apart: 3, of which 1 were waited for; matrix products, arithmetic and copies ran while one was open for 1% of the time, Pallas kernels for 0%

commit v1 on v0

--- a/solution.py
+++ b/solution.py
@@ -22,7 +22,7 @@
     local_terms = lax.dot_general(
         masked, vectors, (((0,), (0,)), ((), ())), preferred_element_type=jnp.float32
     )
-    projected = lax.psum(local_terms, ("row", "col"))
+    projected = jax.lax.psum(jax.lax.psum(local_terms, "row"), "col")
     coupled = jnp.dot(
         weighted.astype(jnp.float32),
         projected,

time: 255 us -> 309 us (1.21)
  waiting for transfers between devices: 220 us -> 276 us
    all_gather x1, waiting for transfers between devices: 0.01 us -> 110 us  [body(): lax.all_gather(masked, 'row', axis=0, tiled=True)]
    psum x1 -> x2, waiting for transfers between devices: 219 us -> 135 us  [body(): projected = jax.lax.psum(jax.lax.psum(local_terms, 'row'), 'col')]
    all_gather x1, waiting for transfers between devices: 0.01 us -> 28.9 us  [body(): row_block = lax.all_gather(weighted, 'col', axis=0, tiled=True)]
  transfers between devices with their start and end apart: 3 -> 4, of which waited for: 1 -> 4; matrix products, arithmetic and copies ran while one was open for 1% -> 1% of each run, Pallas kernels for 0% -> 0%
where the time goes in v1:
time: 309 us
  waiting for transfers between devices  276 us (89%)
  matrix products  15.6 us (5%)
  between operations  13.8 us (4%)
  other arithmetic  3.17 us (1%)
    psum x2, waiting for transfers between devices, body(): projected = jax.lax.psum(jax.lax.psum(local_terms, 'row'), 'col')  135 us
    all_gather x1, waiting for transfers between devices, body(): lax.all_gather(masked, 'row', axis=0, tiled=True)  110 us
    all_gather x1, waiting for transfers between devices, body(): row_block = lax.all_gather(weighted, 'col', axis=0, tiled=True)  28.9 us
    dot_general x1, matrix products, body(): lax.dot_general(row_block, lax.all_gather(masked, 'row', axis=0, tiled=Tr...  10.4 us
  transfers between devices with their start and end apart: 4, of which 4 were waited for; matrix products, arithmetic and copies ran while one was open for 1% of the time, Pallas kernels for 0%

profile of v1, /device:TPU:0, one launch (start us, length us, event | category | flops | bytes accessed | tf_op | source)
XLA Modules:
  0.0 308.7 jit_solution(5598707812487075882)
XLA Ops:
  7.2 0.0 copy-start.2
  7.2 0.0 all-reduce.3.cloned.1.call-start
  7.2 0.7 iota_compare_fusion
  7.9 0.1 lt.18
  8.0 2.4 multiply_convert_fusion
  10.5 0.0 copy-start
  10.5 0.0 copy-done.2
  10.5 1.8 fusion.1
  12.3 0.0 copy-start.3
  12.3 0.0 copy-start.1
  12.3 0.0 all-reduce.3.cloned.1.call-update
  12.3 0.0 all-reduce.5.cloned.1.call-start
  12.4 92.1 %all-reduce.3.cloned.1.call-done = f32[3072,64]{1,0:T(8,128)} async-done(((f32[3072,64]{1,0:T(8,128)}), f32[3072,64]{1,0:T(8,128)}) %all-reduce.3.cloned.1.call-update) | async-done | bytes 786448 | tf_op jit(solution)/shard_map/psum | solution.py:25
  104.5 0.0 all-reduce.5.cloned.1.call-update
  104.5 0.0 copy-done
  104.5 0.0 all-gather.3.cloned.1.call-start
  104.6 0.7 all-gather.3.cloned.1.call-update
  105.2 0.0 all-gather.5.cloned.1.call-start
  105.3 0.5 all-gather.5.cloned.1.call-update
  105.8 0.0 copy-done.3
  105.8 43.2 %all-reduce.5.cloned.1.call-done = f32[3072,64]{1,0:T(8,128)} async-done(((f32[3072,64]{1,0:T(8,128)}), f32[3072,64]{1,0:T(8,128)}) %all-reduce.5.cloned.1.call-update) | async-done | bytes 786448 | tf_op jit(solution)/shard_map/psum | solution.py:25
  149.0 0.0 copy-done.1
  149.0 3.5 %convolution_add_fusion = f32[144,64]{0,1:T(8,128)} fusion(bf16[144,3072]{1,0:T(8,128)(2,1)S(1)} %copy-done.1, f32[3072,64]{1,0:T(8,128)} %all-reduce.5.cloned.1.call-done, bf16[144,64]{0,1:T(8,128)(2,1)S(1)} %copy-done.2, f32[144]{0:T(256)S(1)} %broadcast_select_fusion.1), kind=kOutput, calls=%fused_computation.1 | convolution fusion | flops 339766272 | bytes 1727040 | tf_op jit(solution)/shard_map/dot_general | solution.py:26
  152.5 28.9 %all-gather.3.cloned.1.call-done = bf16[576,3072]{1,0:T(8,128)(2,1)} async-done(((bf16[144,3072]{1,0:T(8,128)(2,1)}), bf16[576,3072]{1,0:T(8,128)(2,1)}) %all-gather.3.cloned.1.call-update) | async-done | bytes 3538960 | tf_op jit(solution)/shard_map/all_gather | solution.py:15
  181.4 110.4 %all-gather.5.cloned.1.call-done = bf16[1152,3072]{1,0:T(8,128)(2,1)} async-done(((bf16[144,3072]{1,0:T(8,128)(2,1)}), bf16[1152,3072]{1,0:T(8,128)(2,1)}) %all-gather.5.cloned.1.call-update) | async-done | bytes 7077904 | tf_op jit(solution)/shard_map/all_gather | solution.py:18
  291.8 10.4 %fusion = f32[576,1152]{1,0:T(8,128)} fusion(bf16[576,3072]{1,0:T(8,128)(2,1)} %all-gather.3.cloned.1.call-done, bf16[1152,3072]{1,0:T(8,128)(2,1)} %all-gather.5.cloned.1.call-done), kind=kOutput, calls=%fused_computation.5 | convolution fusion | flops 4076863488 | bytes 13271040 | tf_op jit(solution)/shard_map/dot_general | solution.py:16
  (1 shorter events, 0.0 us)
Async XLA Ops:
  7.2 3.3 %copy-start.2 = (bf16[144,64]{0,1:T(8,128)(2,1)S(1)}, bf16[144,64]{0,1:T(8,128)(2,1)}, u32[]{:S(2)}) copy-start(bf16[144,64]{0,1:T(8,128)(2,1)} %param.9) | copy-start | bytes 55300
  7.2 97.3 %all-reduce.3.cloned.1.call-start = ((), (), s32[]{:S(2)}) async-start(), calls=%async_computation.2 | async-start | bytes 3145728 | tf_op jit(solution)/shard_map/psum | solution.py:25
  10.5 94.0 %copy-start = (bf16[144,3072]{1,0:T(8,128)(2,1)}, bf16[144,3072]{1,0:T(8,128)(2,1)S(1)}, u32[]{:S(2)}) copy-start(bf16[144,3072]{1,0:T(8,128)(2,1)S(1)} %get-tuple-element.3) | copy-start | bytes 2654212
  12.3 93.5 %copy-start.3 = (f32[144]{0:T(256)S(1)}, f32[144]{0:T(256)}, u32[]{:S(2)}) copy-start(f32[144]{0:T(256)} %param.8) | copy-start | bytes 1732
  12.3 136.7 %copy-start.1 = (bf16[144,3072]{1,0:T(8,128)(2,1)S(1)}, bf16[144,3072]{1,0:T(8,128)(2,1)}, u32[]{:S(2)}) copy-start(bf16[144,3072]{1,0:T(8,128)(2,1)} %get-tuple-element.2) | copy-start | bytes 2654212
  12.3 136.7 %all-reduce.5.cloned.1.call-start = ((), (), s32[]{:S(2)}) async-start(), calls=%async_computation.3 | async-start | bytes 3145728 | tf_op jit(solution)/shard_map/psum | solution.py:25
  104.5 76.9 %all-gather.3.cloned.1.call-start = ((), (), s32[]{:S(2)}) async-start(), calls=%async_computation | async-start | bytes 4423680 | tf_op jit(solution)/shard_map/all_gather | solution.py:15
  105.2 186.5 %all-gather.5.cloned.1.call-start = ((), (), s32[]{:S(2)}) async-start(), calls=%async_computation.1 | async-start | bytes 7962624 | tf_op jit(solution)/shard_map/all_gather | solution.py:18
Sparse Core Ops, SparseCore 0:
  12.4 91.9 all-reduce.2
  106.8 42.1 all-reduce.4
  150.6 30.7 all-gather.2
  183.5 108.2 all-gather.4
